TPU v7x, 32 devices: a whole 2x2x4 slice. The times are simulated.
32 devices in a mesh: row: 16 (over z, y, core), col: 2 (over x).
Axes of the slice: x: 2, y: 2, z: 4, core: 2. Of those that a mesh axis runs over, the one named last changes fastest.
Arguments:
- eigvec: float32 [65536, 1024], P('row', 'col'), may hold values from -6 to 6
- reflectors: float32 [16, 2, 1024, 256], P('row', 'col'), may hold values from -0.125 to 0.125
- tfactors: float32 [16, 2, 256, 256], P('row', 'col'), may hold values from -1 to 1, as said below
- offsets: int32 [2, 16], replicated, may hold values from 3072 to 3584
- owners: int32 [2, 16], replicated, may hold values from 0 to 1
Outputs:
- result: float32 [65536, 1024], P('row', 'col')
Inputs may be any that keep to these rules, and one draw needn't show every extreme that they name: `tfactors`: every factor block is zero below its diagonal.
All inputs are finite; a program needn't handle non-finite values.
Results may differ from a plain program's by a relative error of at most 0.0003.
Values sent between devices are 32-bit elements; how exact they have to be, the bound alone decides.
A program may use at most 64 MiB of HBM per device.

v0:
```python
import functools

import jax
import jax.numpy as jnp
from jax import lax
from jax.experimental import pallas as pl
from jax.experimental.pallas import tpu as pltpu
from jax.sharding import PartitionSpec as P

WIN = 1024
TICKS = 2
CHUNK = 256
PAD = 8
SUB = 8
LARGE = 56
FUSED = 55


def from_root(block, axis, owner):
    block = jnp.where(lax.axis_index(axis) == owner, block, jnp.zeros_like(block))
    return lax.psum(block, axis)


def from_behind(shard, axis, by):
    count = lax.axis_size(axis)
    pairs = [(i, i + by) for i in range(count) if 0 <= i + by < count]
    return lax.ppermute(shard, axis, pairs)


def positions(n):
    return lax.broadcasted_iota(jnp.int32, (n, n), 0), lax.broadcasted_iota(jnp.int32, (n, n), 1)


def fold(factor):
    half = factor.shape[0] // 2
    r, c = positions(half)
    first, side, second = factor[:half, :half], factor[:half, half:], factor[half:, half:]
    both = jnp.where(r <= c, first, second.T)
    diagonal = jnp.sum(jnp.where(r == c, second, 0.0), axis=0, keepdims=True)
    tail = jnp.pad(diagonal, ((0, PAD - 1), (0, half)))
    return jnp.concatenate([jnp.concatenate([both, side], 1), tail], 0)


def unfold(packed):
    half = packed.shape[1] // 2
    r, c = positions(half)
    both, side, diagonal = packed[:half, :half], packed[:half, half:], packed[half : half + 1, :half]
    first = jnp.where(r <= c, both, 0.0)
    second = jnp.where(r < c, both.T, jnp.where(r == c, jnp.broadcast_to(diagonal, both.shape), 0.0))
    return jnp.concatenate(
        [jnp.concatenate([first, side], 1), jnp.concatenate([jnp.zeros_like(first), second], 1)], 0
    )


def split(x):
    high = x.astype(jnp.bfloat16)
    return high, (x - high.astype(jnp.float32)).astype(jnp.bfloat16)


def product(left, right):
    (lh, ll), (rh, rl) = left, right
    return jnp.dot(
        jnp.concatenate([lh, lh, ll], 1),
        jnp.concatenate([rh, rl, rh], 0),
        preferred_element_type=jnp.float32,
    )


def tiles(x):
    return x.reshape(x.shape[0] // SUB, SUB, x.shape[1])


def rows_from(x, shift):
    turned = pltpu.roll(tiles(x), lax.rem(SUB - shift, SUB), axis=1)
    place = lax.broadcasted_iota(jnp.int32, turned[1:].shape, 1)
    return jnp.where(place + shift < SUB, turned[:-1], turned[1:]).reshape(x.shape[0] - SUB, x.shape[1])


def rows_at(x, shift):
    turned = pltpu.roll(tiles(x), shift, axis=1)
    none = jnp.zeros_like(turned[:1])
    ahead, behind = jnp.concatenate([turned, none], 0), jnp.concatenate([none, turned], 0)
    place = lax.broadcasted_iota(jnp.int32, ahead.shape, 1)
    return jnp.where(place >= shift, ahead, behind).reshape(x.shape[0] + SUB, x.shape[1])


def copy_kernel(width, x_ref, held, head, *uppers):
    step = x_ref.shape[0]
    at = pl.program_id(0)
    first = pl.num_programs(0) - WIN // step
    held[...] = x_ref[...]

    @pl.when(at == 0)
    def _():
        head[...] = x_ref[...]

    for part in range(WIN // step):

        @pl.when(at == first + part)
        def _():
            for chunk, upper in enumerate(uppers):
                upper[part * step : (part + 1) * step, :] = x_ref[:, chunk * width : (chunk + 1) * width]


def cost(flops, values):
    return pl.CostEstimate(flops=flops, bytes_accessed=4 * values, transcendentals=0)


def grant(mib):
    return pltpu.CompilerParams(vmem_limit_bytes=mib * 2**20)


def whole(shape):
    return pl.BlockSpec(shape, lambda i: (0,) * len(shape))


def copy_slab(eigvec, half, width):
    rows, cols = eigvec.shape
    count = cols // width
    rolling = pl.BlockSpec((half, cols), lambda i: (i, 0))
    return pl.pallas_call(
        functools.partial(copy_kernel, width),
        grid=(rows // half,),
        in_specs=[rolling],
        out_specs=[rolling, whole((half, cols))] + [whole((WIN, width))] * count,
        out_shape=[jax.ShapeDtypeStruct(eigvec.shape, jnp.float32), jax.ShapeDtypeStruct((half, cols), jnp.float32)]
        + [jax.ShapeDtypeStruct((WIN, width), jnp.float32)] * count,
        cost_estimate=cost(0, (2 * rows + half + WIN) * cols),
        compiler_params=grant(LARGE),
    )(eigvec)


def window_kernel(plan, va, vb, ta, tb, upper, lower, up_out, low_out, frame):
    end = WIN + lower.shape[0]
    frame[:WIN, :] = upper[...]
    frame[WIN:end, :] = lower[...]
    frame[end:, :] = jnp.zeros_like(frame[end:, :])
    for tick in range(TICKS):
        begin, second = plan[0, tick], plan[1, tick] > 0
        block = jnp.where(second, vb[...], va[...])
        vectors = split(block)
        factor = split(unfold(jnp.where(second, tb[...], ta[...])))
        shift = lax.rem(begin, SUB)
        near = pl.ds(pl.multiple_of(begin - shift, SUB), WIN + SUB)
        window = rows_from(frame[near, :], shift)
        coefficients = product(split(block.T), split(window))
        scaled = product(factor, split(coefficients))
        frame[near, :] -= rows_at(product(vectors, split(scaled)), shift)
    up_out[...] = frame[:WIN, :]
    low_out[...] = frame[WIN:end, :]


def apply_window(plan, va, vb, ta, tb, upper, lower, chunk):
    width = upper.shape[1]
    low = lower.shape[0]
    block = va.shape[1]
    return pl.pallas_call(
        window_kernel,
        grid=(1,),
        in_specs=[pl.BlockSpec(memory_space=pltpu.SMEM)] + [whole(x.shape) for x in (va, vb, ta, tb, upper)]
        + [pl.BlockSpec((low, width), lambda i: (0, chunk))],
        out_specs=[whole((WIN, width)), whole((low, width))],
        out_shape=[
            jax.ShapeDtypeStruct((WIN, width), jnp.float32),
            jax.ShapeDtypeStruct((low, width), jnp.float32),
        ],
        scratch_shapes=[pltpu.VMEM((WIN + low + SUB, width), jnp.float32)],
        cost_estimate=cost(3 * TICKS * 2 * width * block * (2 * WIN + block), 2 * WIN * block + 4 * WIN * width),
        compiler_params=grant(60),
    )(plan, va, vb, ta, tb, upper, lower)


def store_kernel(*refs):
    *parts, held, out = refs
    for chunk, part in enumerate(parts):
        width = part.shape[1]
        out[:, chunk * width : (chunk + 1) * width] = part[...]


def store_upper(parts, held):
    rows, cols = held.shape
    return pl.pallas_call(
        store_kernel,
        grid=(1,),
        in_specs=[whole(part.shape) for part in parts] + [pl.BlockSpec(memory_space=pltpu.HBM)],
        out_specs=pl.BlockSpec((WIN, cols), lambda i: (rows // WIN - 1, 0)),
        out_shape=jax.ShapeDtypeStruct(held.shape, jnp.float32),
        input_output_aliases={len(parts): 0},
        cost_estimate=cost(0, 2 * WIN * cols),
        compiler_params=grant(12),
    )(*parts, held)


def top_kernel(first, top, head, held, out):
    out[...] = jnp.where(first[0] > 0, head[...], top[...])


def store_top(first, top, head, held, chunk):
    half, width = top.shape
    return pl.pallas_call(
        top_kernel,
        grid=(1,),
        in_specs=[
            pl.BlockSpec(memory_space=pltpu.SMEM),
            whole(top.shape),
            pl.BlockSpec((half, width), lambda i: (0, chunk)),
            pl.BlockSpec(memory_space=pltpu.HBM),
        ],
        out_specs=pl.BlockSpec((half, width), lambda i: (0, chunk)),
        out_shape=jax.ShapeDtypeStruct(held.shape, jnp.float32),
        input_output_aliases={3: 0},
        cost_estimate=cost(0, 3 * half * width),
        compiler_params=grant(4),
    )(first, top, head, held)


PIECES = 4
PART = 256
MESH = pl.DeviceIdType.MESH


def triple(left, right):
    (lh, ll), (rh, rl) = left, right
    return jnp.dot(
        jnp.concatenate([lh, lh, ll], 1),
        jnp.concatenate([rh, rl, rh], 0),
        preferred_element_type=jnp.float32,
    )


def shifted(ref, start, count, cols):
    tile = lax.div(start, SUB)
    return rows_from(ref[pl.ds(tile * SUB, count + SUB), cols], start - tile * SUB)


def fused_kernel(
    x, v, t, offsets, owners, out,
    frame, v_own, v_far, t_own, t_out, t_far, vh, vl, vth, vtl, th, tl, wh, wl, later, p0, u0, u1, low,
    near_sem, v_sent, v_got, t_sent, t_got, low_sent, low_got, back_sent, back_got,
):
    rows, cols = x.shape
    half, block = WIN // 2, v.shape[3]
    quarter = block // 2
    base = rows - WIN
    row, col = lax.axis_index("row"), lax.axis_index("col")
    last = lax.axis_size("row") - 1
    has_above, has_below = row > 0, row < last
    other = {"col": 1 - col}
    parts = [slice(c, c + PART) for c in range(0, cols, PART)]
    step = WIN // PIECES

    def local(src, dst, which):
        return pltpu.make_async_copy(src, dst, near_sem.at[which])

    def remote(src, dst, sent, got, target):
        return pltpu.make_async_remote_copy(
            src_ref=src, dst_ref=dst, send_sem=sent, recv_sem=got, device_id=target, device_id_type=MESH
        )

    load_t = local(t.at[0, 0], t_own, 0)
    load_v = local(v.at[0, 0], v_own, 1)
    load_upper = local(x.at[pl.ds(base, WIN)], frame.at[pl.ds(0, WIN)], 2)
    load_middle = local(x.at[pl.ds(half, base - half)], out.at[pl.ds(half, base - half)], 3)
    load_head = local(x.at[pl.ds(0, half)], out.at[pl.ds(0, half)], 4)
    send_v = [
        remote(v.at[0, 0, pl.ds(k * step, step)], v_far.at[pl.ds(k * step, step)], v_sent.at[k], v_got.at[k], other)
        for k in range(PIECES)
    ]
    send_t = remote(t_out, t_far, t_sent, t_got, other)
    send_low = remote(x.at[pl.ds(0, half)], frame.at[pl.ds(WIN, half)], low_sent, low_got, {"row": row - 1})
    send_back = [
        remote(low.at[:, pl.ds(c * PART, PART)], out.at[pl.ds(0, half), pl.ds(c * PART, PART)],
               back_sent.at[c], back_got.at[c], {"row": row + 1})
        for c in range(len(parts))
    ]

    load_t.start()
    barrier = pltpu.get_barrier_semaphore()
    pl.semaphore_signal(barrier, inc=1, device_id=other, device_id_type=MESH)

    @pl.when(has_above)
    def _():
        pl.semaphore_signal(barrier, inc=1, device_id={"row": row - 1}, device_id_type=MESH)

    @pl.when(has_below)
    def _():
        pl.semaphore_signal(barrier, inc=1, device_id={"row": row + 1}, device_id_type=MESH)

    load_v.start()
    load_upper.start()

    @pl.when(has_above & has_below)
    def _():
        pl.semaphore_wait(barrier, 3)

    @pl.when(jnp.logical_not(has_above & has_below))
    def _():
        pl.semaphore_wait(barrier, 2)

    send_v[0].start()

    @pl.when(has_above)
    def _():
        send_low.start()

    load_middle.start()

    @pl.when(jnp.logical_not(has_above))
    def _():
        load_head.start()

    load_t.wait()
    factor = t_own[...]
    r, c = positions(quarter)
    first, second = factor[:quarter, :quarter], factor[quarter:, quarter:]
    diagonal = jnp.sum(jnp.where(r == c, second, 0.0), axis=0, keepdims=True)
    t_out[:quarter, :quarter] = jnp.where(r <= c, first, second.T)
    t_out[:quarter, quarter:] = factor[:quarter, quarter:]
    t_out[quarter:, :] = jnp.broadcast_to(jnp.concatenate([diagonal, diagonal], 1), (PAD, block))
    th[0], tl[0] = split(factor)
    send_t.start()
    for k in range(1, PIECES):
        send_v[k].start()

    def prepare(source, holder, k):
        span = slice(k * step, (k + 1) * step)
        piece = source[span, :]
        vh[holder, span, :], vl[holder, span, :] = split(piece)
        vth[holder, :, span], vtl[holder, :, span] = split(piece.T)

    load_v.wait()
    for k in range(PIECES):
        prepare(v_own, 0, k)

    begin = [jnp.clip(offsets[tick, row] - base, 0, half) for tick in range(TICKS)]
    holder = [(owners[tick, row] != col).astype(jnp.int32) for tick in range(TICKS)]
    for u in (u0, u1):
        u[:half, :] = jnp.zeros((half, cols), jnp.float32)
        u[half + WIN :, :] = jnp.zeros((half + SUB, cols), jnp.float32)
    frame[WIN + half :, :] = jnp.zeros((SUB, cols), jnp.float32)

    @pl.when(jnp.logical_not(has_below))
    def _():
        frame[WIN : WIN + half, :] = jnp.zeros((half, cols), jnp.float32)

    load_upper.wait()

    @pl.when(has_below)
    def _():
        send_low.wait_recv()

    def windows(k, carry):
        span = pl.ds(pl.multiple_of(k * 128, 128), 128)
        wh[span, :], wl[span, :] = split(shifted(frame, begin[0] + k * 128, 128, slice(None)))
        later[span, :] = shifted(frame, begin[1] + k * 128, 128, slice(None))
        return carry

    lax.fori_loop(0, WIN // 128, windows, 0)

    send_t.wait_recv()
    th[1], tl[1] = split(unfold(t_far[...]))

    for k in range(PIECES):
        send_v[k].wait_recv()
        prepare(v_far, 1, k)
        span = slice(k * step, (k + 1) * step)
        left = vth[holder[0], :, span], vtl[holder[0], :, span]
        for part in parts:
            sums = triple(left, (wh[span, part], wl[span, part]))
            p0[:, part] = sums if k == 0 else p0[:, part] + sums

    factors = [(th[holder[tick]], tl[holder[tick]]) for tick in range(TICKS)]
    scaled = []
    for c, part in enumerate(parts):
        first = split(triple(factors[0], split(p0[:, part])))
        u0[half : half + WIN, part] = triple((vh[holder[0]], vl[holder[0]]), first)
        window = later[:, part] - shifted(u0, half + begin[1] - begin[0], WIN, part)
        sums = triple((vth[holder[1]], vtl[holder[1]]), split(window))
        second = split(triple(factors[1], split(sums)))
        scaled.append(second)
        u1[WIN : half + WIN, part] = triple((vh[holder[1], half:, :], vl[holder[1], half:, :]), second)
        low[:, part] = (
            frame[WIN : WIN + half, part]
            - shifted(u0, WIN + half - begin[0], half, part)
            - shifted(u1, WIN + half - begin[1], half, part)
        )

        @pl.when(has_below)
        def _():
            send_back[c].start()

    for c, part in enumerate(parts):
        u1[half:WIN, part] = triple((vh[holder[1], :half, :], vl[holder[1], :half, :]), scaled[c])

        def upper(k, carry):
            span = pl.ds(pl.multiple_of(k * 128, 128), 128)
            out[pl.ds(pl.multiple_of(base + k * 128, 128), 128), part] = (
                frame[span, part]
                - shifted(u0, half - begin[0] + k * 128, 128, part)
                - shifted(u1, half - begin[1] + k * 128, 128, part)
            )
            return carry

        lax.fori_loop(0, WIN // 128, upper, 0)

    load_middle.wait()

    @pl.when(jnp.logical_not(has_above))
    def _():
        load_head.wait()

    send_t.wait_send()
    for k in range(PIECES):
        send_v[k].wait_send()

    @pl.when(has_above)
    def _():
        send_low.wait_send()
        for copy in send_back:
            copy.wait_recv()

    @pl.when(has_below)
    def _():
        for copy in send_back:
            copy.wait_send()


def fused(eigvec, reflectors, tfactors, offsets, owners):
    _, cols = eigvec.shape
    block = reflectors.shape[3]
    half = WIN // 2
    parts = cols // PART
    f32, bf16 = jnp.float32, jnp.bfloat16
    dma = pltpu.SemaphoreType.DMA
    arrays = [pltpu.with_memory_space_constraint(a, pltpu.HBM) for a in (eigvec, reflectors, tfactors)]
    return pl.pallas_call(
        fused_kernel,
        in_specs=[pl.BlockSpec(memory_space=pltpu.HBM)] * 3 + [pl.BlockSpec(memory_space=pltpu.SMEM)] * 2,
        out_specs=pl.BlockSpec(memory_space=pltpu.VMEM),
        out_shape=pltpu.VMEM(eigvec.shape, f32),
        scratch_shapes=[
            pltpu.VMEM((WIN + half + SUB, cols), f32),
            pltpu.VMEM((WIN, block), f32),
            pltpu.VMEM((WIN, block), f32),
            pltpu.VMEM((block, block), f32),
            pltpu.VMEM((block // 2 + PAD, block), f32),
            pltpu.VMEM((block // 2 + PAD, block), f32),
            pltpu.VMEM((2, WIN, block), bf16),
            pltpu.VMEM((2, WIN, block), bf16),
            pltpu.VMEM((2, block, WIN), bf16),
            pltpu.VMEM((2, block, WIN), bf16),
            pltpu.VMEM((2, block, block), bf16),
            pltpu.VMEM((2, block, block), bf16),
            pltpu.VMEM((WIN, cols), bf16),
            pltpu.VMEM((WIN, cols), bf16),
            pltpu.VMEM((WIN, cols), f32),
            pltpu.VMEM((block, cols), f32),
            pltpu.VMEM((2 * WIN + SUB, cols), f32),
            pltpu.VMEM((2 * WIN + SUB, cols), f32),
            pltpu.VMEM((half, cols), f32),
            dma((5,)),
            dma((PIECES,)),
            dma((PIECES,)),
            dma,
            dma,
            dma,
            dma,
            dma((parts,)),
            dma((parts,)),
        ],
        cost_estimate=cost(10**10, 10**7),
        compiler_params=pltpu.CompilerParams(collective_id=0, has_side_effects=True, vmem_limit_bytes=FUSED * 2**20),
    )(*arrays, offsets, owners)


def per_device(eigvec, reflectors, tfactors, offsets, owners):
    rows, cols = eigvec.shape
    half = WIN // 2
    width = min(CHUNK, cols)
    own_row = lax.axis_index("row")
    holders = lax.axis_size("col")
    if holders == 2:
        return fused(eigvec, reflectors, tfactors, offsets, owners)
    vectors, factor = reflectors[0, 0], tfactors[0, 0]
    packed = fold(factor)
    source = lax.dynamic_slice_in_dim(owners, own_row, 1, 1)[:, 0]
    begin = lax.dynamic_slice_in_dim(offsets, own_row, 1, 1)[:, 0] - (rows - WIN)
    va, vb = (from_root(vectors, "col", source[t]) for t in range(TICKS))
    ta, tb = (from_root(packed, "col", source[t]) for t in range(TICKS))
    second = jnp.arange(TICKS, dtype=jnp.int32)
    plan = jnp.stack([begin, second])
    result, head, *uppers = copy_slab(eigvec, half, width)
    lower = from_behind(head, "row", -1)
    parts, tops = [], []
    for chunk, upper in enumerate(uppers):
        part, low = apply_window(plan, va, vb, ta, tb, upper, lower, chunk)
        parts.append(part)
        tops.append(from_behind(low, "row", 1))
    result = store_upper(parts, result)
    first = (own_row == 0).astype(jnp.int32)[None]
    for chunk, top in enumerate(tops):
        result = store_top(first, top, head, result, chunk)
    return result


def solution(mesh):
    return jax.shard_map(
        per_device,
        mesh=mesh,
        in_specs=(
            P("row", "col"),
            P("row", "col", None, None),
            P("row", "col", None, None),
            P(),
            P(),
        ),
        out_specs=P("row", "col"),
        check_vma=False,
    )
```

profile of v0, /device:TPU:24, one launch (start us, length us, event | category | flops | bytes accessed | tf_op | source)
XLA Modules:
  0.0 50.4 jit_solution(11750966188457874927)
XLA Ops:
  0.0 47.0 %shard_map.55 = f32[4096,512]{1,0:T(8,128)S(1)} custom-call(f32[4096,512]{1,0:T(8,128)} %x.1, f32[1,1,1024,256]{3,2,1,0:T(8,128)} %v.1, f32[1,1,256,256]{3,2,1,0:T(8,128)} %t.1, s32[2,16]{1,0:T(2,128)} %offsets.1, s32[2,16]{1,0:T(2,128)} %owners.1), custom_call_target="tpu_custom_call" | custom-call | flops 10000000000 | bytes 40000000 | tf_op jit(solution)/shard_map/pallas_call | solution.py:436
  47.0 3.4 %copy.7 = f32[4096,512]{1,0:T(8,128)} copy(f32[4096,512]{1,0:T(8,128)S(1)} %shard_map.55) | data formatting | bytes 16777216
where the time goes:
time: 50.6 us; the launch traced here: 50.4 us
  Pallas kernels  47 us (93%)
  local copies, waits for them, and re-layouts  3.4 us (7%)
    pallas_call x1, Pallas kernels, fused(): pl.pallas_call(fused_kernel, in_specs=[pl.BlockSpec(memory_space=pltpu.HB...  47 us
    unnamed x1, local copies, waits for them, and re-layouts  3.4 us

commit v1 on v0

--- a/solution.py
+++ b/solution.py
@@ -214,7 +214,7 @@
     )(first, top, head, held)
 
 
-PIECES = 4
+PIECE = 64
 PART = 256
 MESH = pl.DeviceIdType.MESH
 
@@ -235,8 +235,9 @@
 
 def fused_kernel(
     x, v, t, offsets, owners, out,
-    frame, v_own, v_far, t_own, t_out, t_far, vh, vl, vth, vtl, th, tl, wh, wl, later, p0, u0, u1, low,
-    near_sem, v_sent, v_got, t_sent, t_got, low_sent, low_got, back_sent, back_got,
+    frame, vectors, t_own, t_out, t_far, vt_out, vt_far, vh, vl, vth, vtl, th, tl, wh, wl, p, c, u0, u1,
+    above, ah, al, ac, n0, n1,
+    near_sem, x_sent, x_got, low_sent, low_got, y_sent, y_got,
 ):
     rows, cols = x.shape
     half, block = WIN // 2, v.shape[3]
@@ -245,9 +246,11 @@
     row, col = lax.axis_index("row"), lax.axis_index("col")
     last = lax.axis_size("row") - 1
     has_above, has_below = row > 0, row < last
-    other = {"col": 1 - col}
-    parts = [slice(c, c + PART) for c in range(0, cols, PART)]
-    step = WIN // PIECES
+    other, below = {"col": 1 - col}, {"row": row + 1}
+    parts = [slice(at, at + PART) for at in range(0, cols, PART)]
+    pieces = [slice(at, at + PIECE) for at in range(block - PIECE, -1, -PIECE)]
+    count = len(pieces)
+    rests = [(at, half // 2) for at in (0, half // 2)]
 
     def local(src, dst, which):
         return pltpu.make_async_copy(src, dst, near_sem.at[which])
@@ -258,23 +261,44 @@
         )
 
     load_t = local(t.at[0, 0], t_own, 0)
-    load_v = local(v.at[0, 0], v_own, 1)
+    load_v = local(v.at[0, 0], vectors.at[0, pl.ds(half, WIN)], 1)
     load_upper = local(x.at[pl.ds(base, WIN)], frame.at[pl.ds(0, WIN)], 2)
-    load_middle = local(x.at[pl.ds(half, base - half)], out.at[pl.ds(half, base - half)], 3)
-    load_head = local(x.at[pl.ds(0, half)], out.at[pl.ds(0, half)], 4)
-    send_v = [
-        remote(v.at[0, 0, pl.ds(k * step, step)], v_far.at[pl.ds(k * step, step)], v_sent.at[k], v_got.at[k], other)
-        for k in range(PIECES)
+    load_head = local(x.at[pl.ds(0, half)], out.at[pl.ds(0, half)], 3)
+    load_middle = local(x.at[pl.ds(half, base - half)], out.at[pl.ds(half, base - half)], 4)
+    send_rest = [
+        remote(v.at[0, 0, pl.ds(half + at, n)], vectors.at[1, pl.ds(WIN + at, n)], x_sent.at[k], x_got.at[k], other)
+        for k, (at, n) in enumerate(rests)
     ]
-    send_t = remote(t_out, t_far, t_sent, t_got, other)
+    send_t = remote(t_out, t_far, x_sent.at[2], x_got.at[2], other)
+    send_vt = [
+        remote(vt_out.at[pl.ds(piece.start, PIECE)], vt_far.at[pl.ds(piece.start, PIECE)],
+               x_sent.at[3 + k], x_got.at[3 + k], other)
+        for k, piece in enumerate(pieces)
+    ]
     send_low = remote(x.at[pl.ds(0, half)], frame.at[pl.ds(WIN, half)], low_sent, low_got, {"row": row - 1})
-    send_back = [
-        remote(low.at[:, pl.ds(c * PART, PART)], out.at[pl.ds(0, half), pl.ds(c * PART, PART)],
-               back_sent.at[c], back_got.at[c], {"row": row + 1})
-        for c in range(len(parts))
+    pass_own = remote(v.at[0, 0, pl.ds(half, half)], above.at[0], y_sent.at[0], y_got.at[0], below)
+    pass_far = [
+        remote(vectors.at[1, pl.ds(WIN + at, n)], above.at[1, pl.ds(at, n)], y_sent.at[1 + k], y_got.at[1 + k], below)
+        for k, (at, n) in enumerate(rests)
     ]
+    pass_first = [
+        remote(c.at[0, pl.ds(piece.start, PIECE)], ac.at[0, pl.ds(piece.start, PIECE)],
+               y_sent.at[3 + k], y_got.at[3 + k], below)
+        for k, piece in enumerate(pieces)
+    ]
+    pass_second = [
+        remote(c.at[1, :, pl.ds(part.start, PART)], ac.at[1, :, pl.ds(part.start, PART)],
+               y_sent.at[3 + count + k], y_got.at[3 + count + k], below)
+        for k, part in enumerate(parts)
+    ]
+
+    def send_below(copy):
+        @pl.when(has_below)
+        def _():
+            copy.start()
 
     load_t.start()
+    load_v.start()
     barrier = pltpu.get_barrier_semaphore()
     pl.semaphore_signal(barrier, inc=1, device_id=other, device_id_type=MESH)
 
@@ -284,10 +308,10 @@
 
     @pl.when(has_below)
     def _():
-        pl.semaphore_signal(barrier, inc=1, device_id={"row": row + 1}, device_id_type=MESH)
-
-    load_v.start()
+        pl.semaphore_signal(barrier, inc=1, device_id=below, device_id_type=MESH)
+
     load_upper.start()
+    load_head.start()
 
     @pl.when(has_above & has_below)
     def _():
@@ -297,47 +321,55 @@
     def _():
         pl.semaphore_wait(barrier, 2)
 
-    send_v[0].start()
+    for copy in send_rest:
+        copy.start()
 
     @pl.when(has_above)
     def _():
         send_low.start()
 
     load_middle.start()
-
-    @pl.when(jnp.logical_not(has_above))
-    def _():
-        load_head.start()
 
     load_t.wait()
     factor = t_own[...]
-    r, c = positions(quarter)
+    r, l = positions(quarter)
     first, second = factor[:quarter, :quarter], factor[quarter:, quarter:]
-    diagonal = jnp.sum(jnp.where(r == c, second, 0.0), axis=0, keepdims=True)
-    t_out[:quarter, :quarter] = jnp.where(r <= c, first, second.T)
+    diagonal = jnp.sum(jnp.where(r == l, second, 0.0), axis=0, keepdims=True)
+    t_out[:quarter, :quarter] = jnp.where(r <= l, first, second.T)
     t_out[:quarter, quarter:] = factor[:quarter, quarter:]
     t_out[quarter:, :] = jnp.broadcast_to(jnp.concatenate([diagonal, diagonal], 1), (PAD, block))
     th[0], tl[0] = split(factor)
+
+    load_v.wait()
+    vt_out[...] = vectors[0, half:WIN, :].T
     send_t.start()
-    for k in range(1, PIECES):
-        send_v[k].start()
-
-    def prepare(source, holder, k):
-        span = slice(k * step, (k + 1) * step)
-        piece = source[span, :]
-        vh[holder, span, :], vl[holder, span, :] = split(piece)
-        vth[holder, :, span], vtl[holder, :, span] = split(piece.T)
-
-    load_v.wait()
-    for k in range(PIECES):
-        prepare(v_own, 0, k)
+    for copy in send_vt:
+        copy.start()
+
+    def prepare(which, start, n):
+        span = slice(start, start + n)
+        piece = vectors[which, half + start : half + start + n, :]
+        vh[which, span, :], vl[which, span, :] = split(piece)
+        vth[which, :, span], vtl[which, :, span] = split(piece.T)
+
+    for at in range(0, WIN, half // 2):
+        prepare(0, at, half // 2)
 
     begin = [jnp.clip(offsets[tick, row] - base, 0, half) for tick in range(TICKS)]
     holder = [(owners[tick, row] != col).astype(jnp.int32) for tick in range(TICKS)]
+    before = jnp.maximum(row - 1, 0)
+    above_begin = [jnp.clip(offsets[tick, before] - base, 0, half) for tick in range(TICKS)]
+    above_holder = [(owners[tick, before] != col).astype(jnp.int32) for tick in range(TICKS)]
     for u in (u0, u1):
         u[:half, :] = jnp.zeros((half, cols), jnp.float32)
         u[half + WIN :, :] = jnp.zeros((half + SUB, cols), jnp.float32)
+    for n in (n0, n1):
+        n[half:, :] = jnp.zeros((half + SUB, cols), jnp.float32)
+    for which in range(2):
+        vectors[which, :half, :] = jnp.zeros((half, block), jnp.float32)
+        vectors[which, half + WIN :, :] = jnp.zeros((half + SUB, block), jnp.float32)
     frame[WIN + half :, :] = jnp.zeros((SUB, cols), jnp.float32)
+    p[0] = jnp.zeros((block, cols), jnp.float32)
 
     @pl.when(jnp.logical_not(has_below))
     def _():
@@ -348,11 +380,17 @@
     @pl.when(has_below)
     def _():
         send_low.wait_recv()
+        pass_own.start()
+
+    for k, (at, n) in enumerate(rests):
+        send_rest[k].wait_recv()
+        send_below(pass_far[k])
+        prepare(1, half + at, n)
 
     def windows(k, carry):
         span = pl.ds(pl.multiple_of(k * 128, 128), 128)
-        wh[span, :], wl[span, :] = split(shifted(frame, begin[0] + k * 128, 128, slice(None)))
-        later[span, :] = shifted(frame, begin[1] + k * 128, 128, slice(None))
+        for tick in range(TICKS):
+            wh[tick, span, :], wl[tick, span, :] = split(shifted(frame, begin[tick] + k * 128, 128, slice(None)))
         return carry
 
     lax.fori_loop(0, WIN // 128, windows, 0)
@@ -360,37 +398,53 @@
     send_t.wait_recv()
     th[1], tl[1] = split(unfold(t_far[...]))
 
-    for k in range(PIECES):
-        send_v[k].wait_recv()
-        prepare(v_far, 1, k)
-        span = slice(k * step, (k + 1) * step)
-        left = vth[holder[0], :, span], vtl[holder[0], :, span]
+    for k, piece in enumerate(pieces):
+        send_vt[k].wait_recv()
+        vth[1, piece, :half], vtl[1, piece, :half] = split(vt_far[piece, :])
+        for tick in range(TICKS):
+            left = vth[holder[tick], piece, :], vtl[holder[tick], piece, :]
+            for part in parts:
+                p[tick, piece, part] = triple(left, (wh[tick, :, part], wl[tick, :, part]))
+            if tick == 0:
+                left = th[holder[0], piece, :], tl[holder[0], piece, :]
+                for part in parts:
+                    c[0, piece, part] = triple(left, split(p[0, :, part]))
+                send_below(pass_first[k])
+        if piece.start % quarter == 0:
+            span = slice(piece.start, piece.start + quarter)
+            natural = vt_far[span, :].T
+            vectors[1, half:WIN, span] = natural
+            vh[1, :half, span], vl[1, :half, span] = split(natural)
+        if k == 0:
+
+            @pl.when(has_above)
+            def _():
+                pass_own.wait_recv()
+                for copy in pass_far:
+                    copy.wait_recv()
+                for which in range(2):
+                    ah[which], al[which] = split(above[which])
+
+    moved = split(shifted(vectors.at[holder[0]], half + begin[1] - begin[0], WIN, slice(None)))
+    cross = split(triple((vth[holder[1]], vtl[holder[1]]), moved))
+    factor = th[holder[1]], tl[holder[1]]
+    for k, part in enumerate(parts):
+        sums = p[1, :, part] - triple(cross, split(c[0, :, part]))
+        c[1, :, part] = triple(factor, split(sums))
+        send_below(pass_second[k])
+
+    @pl.when(has_above)
+    def _():
+        for copy in pass_first:
+            copy.wait_recv()
         for part in parts:
-            sums = triple(left, (wh[span, part], wl[span, part]))
-            p0[:, part] = sums if k == 0 else p0[:, part] + sums
-
-    factors = [(th[holder[tick]], tl[holder[tick]]) for tick in range(TICKS)]
-    scaled = []
-    for c, part in enumerate(parts):
-        first = split(triple(factors[0], split(p0[:, part])))
-        u0[half : half + WIN, part] = triple((vh[holder[0]], vl[holder[0]]), first)
-        window = later[:, part] - shifted(u0, half + begin[1] - begin[0], WIN, part)
-        sums = triple((vth[holder[1]], vtl[holder[1]]), split(window))
-        second = split(triple(factors[1], split(sums)))
-        scaled.append(second)
-        u1[WIN : half + WIN, part] = triple((vh[holder[1], half:, :], vl[holder[1], half:, :]), second)
-        low[:, part] = (
-            frame[WIN : WIN + half, part]
-            - shifted(u0, WIN + half - begin[0], half, part)
-            - shifted(u1, WIN + half - begin[1], half, part)
-        )
-
-        @pl.when(has_below)
-        def _():
-            send_back[c].start()
-
-    for c, part in enumerate(parts):
-        u1[half:WIN, part] = triple((vh[holder[1], :half, :], vl[holder[1], :half, :]), scaled[c])
+            n0[:half, part] = triple((ah[above_holder[0]], al[above_holder[0]]), split(ac[0, :, part]))
+
+    load_head.wait()
+
+    for part in parts:
+        for tick, u in enumerate((u0, u1)):
+            u[half : half + WIN, part] = triple((vh[holder[tick]], vl[holder[tick]]), split(c[tick, :, part]))
 
         def upper(k, carry):
             span = pl.ds(pl.multiple_of(k * 128, 128), 128)
@@ -404,24 +458,22 @@
         lax.fori_loop(0, WIN // 128, upper, 0)
 
     load_middle.wait()
-
-    @pl.when(jnp.logical_not(has_above))
-    def _():
-        load_head.wait()
-
-    send_t.wait_send()
-    for k in range(PIECES):
-        send_v[k].wait_send()
+    for copy in (*send_rest, send_t, *send_vt):
+        copy.wait_send()
 
     @pl.when(has_above)
     def _():
+        for k, part in enumerate(parts):
+            pass_second[k].wait_recv()
+            n1[:half, part] = triple((ah[above_holder[1]], al[above_holder[1]]), split(ac[1, :, part]))
+            out[:half, part] -= shifted(n0, half - above_begin[0], half, part) + shifted(
+                n1, half - above_begin[1], half, part
+            )
         send_low.wait_send()
-        for copy in send_back:
-            copy.wait_recv()
 
     @pl.when(has_below)
     def _():
-        for copy in send_back:
+        for copy in (pass_own, *pass_far, *pass_first, *pass_second):
             copy.wait_send()
 
 
@@ -429,7 +481,7 @@
     _, cols = eigvec.shape
     block = reflectors.shape[3]
     half = WIN // 2
-    parts = cols // PART
+    count = block // PIECE
     f32, bf16 = jnp.float32, jnp.bfloat16
     dma = pltpu.SemaphoreType.DMA
     arrays = [pltpu.with_memory_space_constraint(a, pltpu.HBM) for a in (eigvec, reflectors, tfactors)]
@@ -440,33 +492,37 @@
         out_shape=pltpu.VMEM(eigvec.shape, f32),
         scratch_shapes=[
             pltpu.VMEM((WIN + half + SUB, cols), f32),
-            pltpu.VMEM((WIN, block), f32),
-            pltpu.VMEM((WIN, block), f32),
+            pltpu.VMEM((2, 2 * WIN + SUB, block), f32),
             pltpu.VMEM((block, block), f32),
             pltpu.VMEM((block // 2 + PAD, block), f32),
             pltpu.VMEM((block // 2 + PAD, block), f32),
+            pltpu.VMEM((block, half), f32),
+            pltpu.VMEM((block, half), f32),
             pltpu.VMEM((2, WIN, block), bf16),
             pltpu.VMEM((2, WIN, block), bf16),
             pltpu.VMEM((2, block, WIN), bf16),
             pltpu.VMEM((2, block, WIN), bf16),
             pltpu.VMEM((2, block, block), bf16),
             pltpu.VMEM((2, block, block), bf16),
-            pltpu.VMEM((WIN, cols), bf16),
-            pltpu.VMEM((WIN, cols), bf16),
-            pltpu.VMEM((WIN, cols), f32),
-            pltpu.VMEM((block, cols), f32),
+            pltpu.VMEM((TICKS, WIN, cols), bf16),
+            pltpu.VMEM((TICKS, WIN, cols), bf16),
+            pltpu.VMEM((TICKS, block, cols), f32),
+            pltpu.VMEM((TICKS, block, cols), f32),
             pltpu.VMEM((2 * WIN + SUB, cols), f32),
             pltpu.VMEM((2 * WIN + SUB, cols), f32),
-            pltpu.VMEM((half, cols), f32),
+            pltpu.VMEM((2, half, block), f32),
+            pltpu.VMEM((2, half, block), bf16),
+            pltpu.VMEM((2, half, block), bf16),
+            pltpu.VMEM((TICKS, block, cols), f32),
+            pltpu.VMEM((WIN + SUB, cols), f32),
+            pltpu.VMEM((WIN + SUB, cols), f32),
             dma((5,)),
-            dma((PIECES,)),
-            dma((PIECES,)),
+            dma((3 + count,)),
+            dma((3 + count,)),
             dma,
             dma,
-            dma,
-            dma,
-            dma((parts,)),
-            dma((parts,)),
+            dma((3 + count + cols // PART,)),
+            dma((3 + count + cols // PART,)),
         ],
         cost_estimate=cost(10**10, 10**7),
         compiler_params=pltpu.CompilerParams(collective_id=0, has_side_effects=True, vmem_limit_bytes=FUSED * 2**20),

time: 50.6 us -> 46.1 us (0.911)
  Pallas kernels: 47 us -> 42.5 us
    pallas_call x1, Pallas kernels: 47 us -> 42.5 us  [fused(): pl.pallas_call(fused_kernel, in_specs=[pl.BlockSpec(memory_space=pltpu.HB...]
where the time goes in v1:
time: 46.1 us; the launch traced here: 46 us
  Pallas kernels  42.5 us (92%)
  local copies, waits for them, and re-layouts  3.4 us (7%)
    pallas_call x1, Pallas kernels, fused(): pl.pallas_call(fused_kernel, in_specs=[pl.BlockSpec(memory_space=pltpu.HB...  42.5 us
    unnamed x1, local copies, waits for them, and re-layouts  3.4 us

profile of v1, /device:TPU:24, one launch (start us, length us, event | category | flops | bytes accessed | tf_op | source)
XLA Modules:
  0.0 46.0 jit_solution(14079669353305550001)
XLA Ops:
  0.0 42.5 %shard_map.55 = f32[4096,512]{1,0:T(8,128)S(1)} custom-call(f32[4096,512]{1,0:T(8,128)} %x.1, f32[1,1,1024,256]{3,2,1,0:T(8,128)} %v.1, f32[1,1,256,256]{3,2,1,0:T(8,128)} %t.1, s32[2,16]{1,0:T(2,128)} %offsets.1, s32[2,16]{1,0:T(2,128)} %owners.1), custom_call_target="tpu_custom_call" | custom-call | flops 10000000000 | bytes 40000000 | tf_op jit(solution)/shard_map/pallas_call | solution.py:488
  42.6 3.4 %copy.7 = f32[4096,512]{1,0:T(8,128)} copy(f32[4096,512]{1,0:T(8,128)S(1)} %shard_map.55) | data formatting | bytes 16777216

commit v2 on v1

--- a/solution.py
+++ b/solution.py
@@ -13,7 +13,8 @@
 PAD = 8
 SUB = 8
 LARGE = 56
-FUSED = 55
+FUSED = 53
+STREAMS = 8
 
 
 def from_root(block, axis, owner):
@@ -234,9 +235,9 @@
 
 
 def fused_kernel(
-    x, v, t, offsets, owners, out,
+    x, v, t, offsets, owners, out, tail, tail_h, tail_l,
     frame, vectors, t_own, t_out, t_far, vt_out, vt_far, vh, vl, vth, vtl, th, tl, wh, wl, p, c, u0, u1,
-    above, ah, al, ac, n0, n1,
+    above, ah, al, ac,
     near_sem, x_sent, x_got, low_sent, low_got, y_sent, y_got,
 ):
     rows, cols = x.shape
@@ -266,7 +267,7 @@
     load_head = local(x.at[pl.ds(0, half)], out.at[pl.ds(0, half)], 3)
     load_middle = local(x.at[pl.ds(half, base - half)], out.at[pl.ds(half, base - half)], 4)
     send_rest = [
-        remote(v.at[0, 0, pl.ds(half + at, n)], vectors.at[1, pl.ds(WIN + at, n)], x_sent.at[k], x_got.at[k], other)
+        remote(vectors.at[0, pl.ds(WIN + at, n)], vectors.at[1, pl.ds(WIN + at, n)], x_sent.at[k], x_got.at[k], other)
         for k, (at, n) in enumerate(rests)
     ]
     send_t = remote(t_out, t_far, x_sent.at[2], x_got.at[2], other)
@@ -275,19 +276,19 @@
                x_sent.at[3 + k], x_got.at[3 + k], other)
         for k, piece in enumerate(pieces)
     ]
-    send_low = remote(x.at[pl.ds(0, half)], frame.at[pl.ds(WIN, half)], low_sent, low_got, {"row": row - 1})
-    pass_own = remote(v.at[0, 0, pl.ds(half, half)], above.at[0], y_sent.at[0], y_got.at[0], below)
+    send_low = remote(out.at[pl.ds(0, half)], frame.at[pl.ds(WIN, half)], low_sent, low_got, {"row": row - 1})
+    pass_own = remote(vectors.at[0, pl.ds(WIN, half)], above.at[0, pl.ds(0, half)], y_sent.at[0], y_got.at[0], below)
     pass_far = [
         remote(vectors.at[1, pl.ds(WIN + at, n)], above.at[1, pl.ds(at, n)], y_sent.at[1 + k], y_got.at[1 + k], below)
         for k, (at, n) in enumerate(rests)
     ]
     pass_first = [
-        remote(c.at[0, pl.ds(piece.start, PIECE)], ac.at[0, pl.ds(piece.start, PIECE)],
+        remote(c.at[0, pl.ds(piece.start, PIECE)], ac.at[pl.ds(piece.start, PIECE)],
                y_sent.at[3 + k], y_got.at[3 + k], below)
         for k, piece in enumerate(pieces)
     ]
     pass_second = [
-        remote(c.at[1, :, pl.ds(part.start, PART)], ac.at[1, :, pl.ds(part.start, PART)],
+        remote(c.at[1, :, pl.ds(part.start, PART)], tail.at[:, pl.ds(part.start, PART)],
                y_sent.at[3 + count + k], y_got.at[3 + count + k], below)
         for k, part in enumerate(parts)
     ]
@@ -297,8 +298,9 @@
         def _():
             copy.start()
 
+    load_v.start()
+    load_head.start()
     load_t.start()
-    load_v.start()
     barrier = pltpu.get_barrier_semaphore()
     pl.semaphore_signal(barrier, inc=1, device_id=other, device_id_type=MESH)
 
@@ -311,7 +313,6 @@
         pl.semaphore_signal(barrier, inc=1, device_id=below, device_id_type=MESH)
 
     load_upper.start()
-    load_head.start()
 
     @pl.when(has_above & has_below)
     def _():
@@ -321,8 +322,11 @@
     def _():
         pl.semaphore_wait(barrier, 2)
 
+    load_v.wait()
     for copy in send_rest:
         copy.start()
+
+    load_head.wait()
 
     @pl.when(has_above)
     def _():
@@ -340,7 +344,6 @@
     t_out[quarter:, :] = jnp.broadcast_to(jnp.concatenate([diagonal, diagonal], 1), (PAD, block))
     th[0], tl[0] = split(factor)
 
-    load_v.wait()
     vt_out[...] = vectors[0, half:WIN, :].T
     send_t.start()
     for copy in send_vt:
@@ -363,11 +366,10 @@
     for u in (u0, u1):
         u[:half, :] = jnp.zeros((half, cols), jnp.float32)
         u[half + WIN :, :] = jnp.zeros((half + SUB, cols), jnp.float32)
-    for n in (n0, n1):
-        n[half:, :] = jnp.zeros((half + SUB, cols), jnp.float32)
     for which in range(2):
         vectors[which, :half, :] = jnp.zeros((half, block), jnp.float32)
         vectors[which, half + WIN :, :] = jnp.zeros((half + SUB, block), jnp.float32)
+        above[which, half:, :] = jnp.zeros((half + SUB, block), jnp.float32)
     frame[WIN + half :, :] = jnp.zeros((SUB, cols), jnp.float32)
     p[0] = jnp.zeros((block, cols), jnp.float32)
 
@@ -375,17 +377,17 @@
     def _():
         frame[WIN : WIN + half, :] = jnp.zeros((half, cols), jnp.float32)
 
+    for copy in send_rest:
+        copy.wait_recv()
+    for copy in (pass_own, *pass_far):
+        send_below(copy)
+    for at, n in rests:
+        prepare(1, half + at, n)
     load_upper.wait()
 
     @pl.when(has_below)
     def _():
         send_low.wait_recv()
-        pass_own.start()
-
-    for k, (at, n) in enumerate(rests):
-        send_rest[k].wait_recv()
-        send_below(pass_far[k])
-        prepare(1, half + at, n)
 
     def windows(k, carry):
         span = pl.ds(pl.multiple_of(k * 128, 128), 128)
@@ -422,8 +424,15 @@
                 pass_own.wait_recv()
                 for copy in pass_far:
                     copy.wait_recv()
-                for which in range(2):
-                    ah[which], al[which] = split(above[which])
+                for tick, (high, rest) in enumerate(((ah, al), (tail_h, tail_l))):
+                    lower = shifted(above.at[above_holder[tick]], half - above_begin[tick], half, slice(None))
+                    high[...], rest[...] = split(lower)
+
+            @pl.when(jnp.logical_not(has_above))
+            def _():
+                tail[...] = jnp.zeros_like(tail)
+                tail_h[...] = jnp.zeros_like(tail_h)
+                tail_l[...] = jnp.zeros_like(tail_l)
 
     moved = split(shifted(vectors.at[holder[0]], half + begin[1] - begin[0], WIN, slice(None)))
     cross = split(triple((vth[holder[1]], vtl[holder[1]]), moved))
@@ -435,12 +444,11 @@
 
     @pl.when(has_above)
     def _():
+        send_low.wait_send()
         for copy in pass_first:
             copy.wait_recv()
         for part in parts:
-            n0[:half, part] = triple((ah[above_holder[0]], al[above_holder[0]]), split(ac[0, :, part]))
-
-    load_head.wait()
+            out[:half, part] -= triple((ah[...], al[...]), split(ac[:, part]))
 
     for part in parts:
         for tick, u in enumerate((u0, u1)):
@@ -463,13 +471,8 @@
 
     @pl.when(has_above)
     def _():
-        for k, part in enumerate(parts):
-            pass_second[k].wait_recv()
-            n1[:half, part] = triple((ah[above_holder[1]], al[above_holder[1]]), split(ac[1, :, part]))
-            out[:half, part] -= shifted(n0, half - above_begin[0], half, part) + shifted(
-                n1, half - above_begin[1], half, part
-            )
-        send_low.wait_send()
+        for copy in pass_second:
+            copy.wait_recv()
 
     @pl.when(has_below)
     def _():
@@ -477,19 +480,43 @@
             copy.wait_send()
 
 
+def finish_kernel(held, tail, tail_h, tail_l, out, top, sems):
+    rows, cols = held.shape
+    half = WIN // 2
+    step = (rows - half) // (STREAMS - 1)
+    copies = []
+    for k in range(STREAMS - 1):
+        span = pl.ds(half + k * step, step)
+        copies.append(pltpu.make_async_copy(held.at[span], out.at[span], sems.at[k]))
+    for copy in copies:
+        copy.start()
+    last = pltpu.make_async_copy(top, out.at[pl.ds(0, half)], sems.at[STREAMS - 1])
+    for at in range(0, cols, PART):
+        part = slice(at, at + PART)
+        top[:, part] = held[:half, part] - triple((tail_h[...], tail_l[...]), split(tail[:, part]))
+    last.start()
+    for copy in (*copies, last):
+        copy.wait()
+
+
 def fused(eigvec, reflectors, tfactors, offsets, owners):
-    _, cols = eigvec.shape
+    rows, cols = eigvec.shape
     block = reflectors.shape[3]
     half = WIN // 2
     count = block // PIECE
     f32, bf16 = jnp.float32, jnp.bfloat16
     dma = pltpu.SemaphoreType.DMA
     arrays = [pltpu.with_memory_space_constraint(a, pltpu.HBM) for a in (eigvec, reflectors, tfactors)]
-    return pl.pallas_call(
+    results = pl.pallas_call(
         fused_kernel,
         in_specs=[pl.BlockSpec(memory_space=pltpu.HBM)] * 3 + [pl.BlockSpec(memory_space=pltpu.SMEM)] * 2,
-        out_specs=pl.BlockSpec(memory_space=pltpu.VMEM),
-        out_shape=pltpu.VMEM(eigvec.shape, f32),
+        out_specs=[pl.BlockSpec(memory_space=pltpu.VMEM)] * 4,
+        out_shape=[
+            pltpu.VMEM(eigvec.shape, f32),
+            pltpu.VMEM((block, cols), f32),
+            pltpu.VMEM((half, block), bf16),
+            pltpu.VMEM((half, block), bf16),
+        ],
         scratch_shapes=[
             pltpu.VMEM((WIN + half + SUB, cols), f32),
             pltpu.VMEM((2, 2 * WIN + SUB, block), f32),
@@ -510,12 +537,10 @@
             pltpu.VMEM((TICKS, block, cols), f32),
             pltpu.VMEM((2 * WIN + SUB, cols), f32),
             pltpu.VMEM((2 * WIN + SUB, cols), f32),
-            pltpu.VMEM((2, half, block), f32),
-            pltpu.VMEM((2, half, block), bf16),
-            pltpu.VMEM((2, half, block), bf16),
-            pltpu.VMEM((TICKS, block, cols), f32),
-            pltpu.VMEM((WIN + SUB, cols), f32),
-            pltpu.VMEM((WIN + SUB, cols), f32),
+            pltpu.VMEM((2, WIN + SUB, block), f32),
+            pltpu.VMEM((half, block), bf16),
+            pltpu.VMEM((half, block), bf16),
+            pltpu.VMEM((block, cols), f32),
             dma((5,)),
             dma((3 + count,)),
             dma((3 + count,)),
@@ -527,6 +552,15 @@
         cost_estimate=cost(10**10, 10**7),
         compiler_params=pltpu.CompilerParams(collective_id=0, has_side_effects=True, vmem_limit_bytes=FUSED * 2**20),
     )(*arrays, offsets, owners)
+    return pl.pallas_call(
+        finish_kernel,
+        in_specs=[pl.BlockSpec(memory_space=pltpu.VMEM)] * 4,
+        out_specs=pl.BlockSpec(memory_space=pltpu.HBM),
+        out_shape=jax.ShapeDtypeStruct(eigvec.shape, f32),
+        scratch_shapes=[pltpu.VMEM((half, cols), f32), dma((STREAMS,))],
+        cost_estimate=cost(0, 2 * rows * cols),
+        compiler_params=grant(8),
+    )(*results)
 
 
 def per_device(eigvec, reflectors, tfactors, offsets, owners):

time: 46.1 us -> 44.8 us (0.972)
  local copies, waits for them, and re-layouts: 3.4 us -> 0 us
  Pallas kernels: 42.5 us -> 44.6 us
    unnamed x1 -> x0, local copies, waits for them, and re-layouts: 3.4 us -> none
    pallas_call x0 -> x1, Pallas kernels: none -> 3.37 us  [fused(): pl.pallas_call(finish_kernel, in_specs=[pl.BlockSpec(memory_space=pltpu.V...]
    pallas_call x1, Pallas kernels: 42.5 us -> 41.2 us  [fused(): pl.pallas_call(fused_kernel, in_specs=[pl.BlockSpec(memory_space=pltpu.HB...]
where the time goes in v2:
time: 44.8 us; the launch traced here: 44.6 us
  Pallas kernels  44.6 us (100%)
    pallas_call x1, Pallas kernels, fused(): pl.pallas_call(fused_kernel, in_specs=[pl.BlockSpec(memory_space=pltpu.HB...  41.2 us
    pallas_call x1, Pallas kernels, fused(): pl.pallas_call(finish_kernel, in_specs=[pl.BlockSpec(memory_space=pltpu.V...  3.37 us

profile of v2, /device:TPU:24, one launch (start us, length us, event | category | flops | bytes accessed | tf_op | source)
XLA Modules:
  0.0 44.6 jit_solution(710119889418806261)
XLA Ops:
  0.0 41.2 %shard_map.55 = (f32[4096,512]{1,0:T(8,128)S(1)}, f32[256,512]{1,0:T(8,128)S(1)}, bf16[512,256]{1,0:T(8,128)(2,1)S(1)}, bf16[512,256]{1,0:T(8,128)(2,1)S(1)}) custom-call(f32[4096,512]{1,0:T(8,128)} %x.1, f32[1,1,1024,256]{3,2,1,0:T(8,128)} %v.1, f32[1,1,256,256]{3,2,1,0:T(8,128)} %t.1, s32[2,16]{1,0:T(2,128)} %offsets.1, s32[2,16]{1,0:T(2,128)} %owners.1), custom_call_target="tpu_custom_call" | custom-call | flops 10000000000 | bytes 40000000 | tf_op jit(solution)/shard_map/pallas_call | solution.py:510
  41.2 3.4 %shard_map.56 = f32[4096,512]{1,0:T(8,128)} custom-call(f32[4096,512]{1,0:T(8,128)S(1)} %get-tuple-element.9.held, f32[256,512]{1,0:T(8,128)S(1)} %get-tuple-element.10.tail, bf16[512,256]{1,0:T(8,128)(2,1)S(1)} %get-tuple-element.11.tail_h, bf16[512,256]{1,0:T(8,128)(2,1)S(1)} %get-tuple-element.12.tail_l), custom_call_target="tpu_custom_call" | custom-call | bytes 16777216 | tf_op jit(solution)/shard_map/pallas_call | solution.py:555
